TPU v7x, 32 devices: a whole 2x2x4 slice. The times are simulated.
32 devices in a mesh: groups: 2 (over y), wide: 8 (over z, x), narrow: 2 (over core).
Axes of the slice: x: 2, y: 2, z: 4, core: 2. Of those that a mesh axis runs over, the one named last changes fastest.
Arguments:
- queries: bfloat16 [4, 2048, 64], P(('groups', 'narrow'), 'wide'), parts along dimension 0, may hold values from -6 to 6
- key_rows: bfloat16 [4, 2048, 64], P(('groups', 'narrow'), 'wide'), parts along dimension 0, may hold values from -6 to 6
- values: bfloat16 [4, 2048, 64], P(('groups', 'narrow'), 'wide'), parts along dimension 0, may hold values from -6 to 6
- log_gate: float32 [4, 2048], P(('groups', 'narrow'), 'wide'), parts along dimension 0, may hold values from -0.8 to 0, as said below
- lengths: int32 [4], P(('groups', 'narrow')), parts along dimension 0, may hold values from 1024 to 2048
- cont_queries: bfloat16 [160, 64], P(('groups', 'wide', 'narrow')), parts along dimension 0, may hold values from -6 to 6
- cont_prompt: int32 [160], P(('groups', 'wide', 'narrow')), parts along dimension 0, may hold values from 0 to 1
Outputs:
- prompt_out: bfloat16 [4, 2048, 64], P(('groups', 'narrow'), 'wide'), parts along dimension 0
- cont_out: bfloat16 [160, 64], P(('groups', 'wide', 'narrow')), parts along dimension 0
There are 2 independent parts, one for each index of `groups`. A program takes and returns all parts, laid end to end along the dimension named above; each array names one. Nothing has to cross between parts.
Inputs may be any that keep to these rules, and one draw needn't show every extreme that they name: `log_gate`: gates only shrink the state: every entry is at most zero.
All inputs are finite; a program needn't handle non-finite values.
Results may differ from a plain program's by a relative error of at most 0.0067.
Values may be sent and summed in bfloat16 or wider, within the bound.
No kernel may reach another device: no remote copies, remote signals or barrier semaphores. Data moves between devices by JAX's collectives and lax.ppermute only.
A program may use at most 64 MiB of HBM per device.

v0:
```python
import jax
import jax.numpy as jnp
import numpy as np
from jax import lax
from jax.sharding import PartitionSpec as P

epsilon = 1e-06
block_rows = 1024


def rms_rows(running):
    return running * lax.rsqrt(jnp.mean(running * running, axis=-1, keepdims=True) + epsilon)


def extend_zeros(table, pad_count):
    return np.concatenate([table, np.zeros((pad_count,), table.dtype)])


def pair_tables(head_width, shard_count):
    lead_index, trail_index = np.triu_indices(head_width)
    doubled = np.where(lead_index == trail_index, 1.0, 2.0)
    feature_count = lead_index.shape[0]
    padded_rows = -(-feature_count // shard_count) * shard_count
    block_width = min(block_rows, padded_rows)
    full_length = -(-padded_rows // block_width) * block_width
    pad_count = full_length - lead_index.shape[0]
    lead_index = extend_zeros(lead_index, pad_count).astype(np.int32)
    trail_index = extend_zeros(trail_index, pad_count).astype(np.int32)
    doubled = extend_zeros(doubled, pad_count).astype(np.float32)
    live_pairs = (doubled > 0).astype(np.float32)
    return (
        jnp.asarray(lead_index),
        jnp.asarray(trail_index),
        jnp.asarray(doubled),
        jnp.asarray(live_pairs),
        padded_rows,
        block_width,
        full_length,
    )


def pair_block(rows, lead_part, trail_part, forget_multiplier):
    leading_columns = jnp.take(rows, lead_part, axis=1).astype(jnp.float32)
    right_cols = jnp.take(rows, trail_part, axis=1).astype(jnp.float32)
    return (leading_columns * right_cols * forget_multiplier[None, :]).astype(jnp.bfloat16)


def block_state(key_rows, spread, tables):
    lead_all, trail_all, doubled_all, live_pairs, padded_rows, block_width, full_length = tables
    head_width = key_rows.shape[1]

    def fill_block(block_index, state):
        first_row = block_index * block_width
        features = pair_block(
            key_rows,
            lax.dynamic_slice_in_dim(lead_all, first_row, block_width),
            lax.dynamic_slice_in_dim(trail_all, first_row, block_width),
            lax.dynamic_slice_in_dim(live_pairs, first_row, block_width),
        )
        state_block = lax.dot_general(
            features, spread, (((0,), (0,)), ((), ())), preferred_element_type=jnp.float32
        )
        return lax.dynamic_update_slice_in_dim(
            state, state_block.astype(jnp.bfloat16), first_row, 0
        )

    initial = jnp.zeros((full_length, head_width), jnp.bfloat16)
    return lax.fori_loop(0, full_length // block_width, fill_block, initial)[:padded_rows]


def carried_read(query_rows, carried, tables):
    lead_all, trail_all, doubled_all, live_pairs, padded_rows, block_width, full_length = tables
    row_count, head_width = query_rows.shape
    if full_length > padded_rows:
        carried = jnp.pad(carried, ((0, full_length - padded_rows), (0, 0)))

    def add_block(block_index, running):
        first_row = block_index * block_width
        features = pair_block(
            query_rows,
            lax.dynamic_slice_in_dim(lead_all, first_row, block_width),
            lax.dynamic_slice_in_dim(trail_all, first_row, block_width),
            lax.dynamic_slice_in_dim(doubled_all, first_row, block_width),
        )
        state_rows = lax.dynamic_slice_in_dim(carried, first_row, block_width, 0)
        return running + jnp.dot(features, state_rows, preferred_element_type=jnp.float32)

    return lax.fori_loop(
        0, full_length // block_width, add_block, jnp.zeros((row_count, head_width), jnp.float32)
    )


def owner_prefix(sent_slices, totals):
    shard_count = totals.shape[0]
    inclusive = jnp.cumsum(totals)
    exclusive = jnp.concatenate([jnp.zeros((1,), jnp.float32), inclusive])
    target = lax.iota(jnp.int32, shard_count + 1)[:, None]
    source = lax.iota(jnp.int32, shard_count)[None, :]
    weight = jnp.exp(jnp.where(source < target, exclusive[:, None] - inclusive[None, :], -jnp.inf))
    return jnp.einsum(
        "wu,urn->wrn", weight, sent_slices.astype(jnp.float32), precision=lax.Precision.HIGHEST
    )


def prompt_rows(query_rows, key_rows, payload_lines, cumulative, live_mask, carried, tables):
    row_count, head_width = query_rows.shape
    scores = lax.dot_general(
        query_rows, key_rows, (((1,), (1,)), ((), ())), preferred_element_type=jnp.float32
    )
    row_ids = lax.iota(jnp.int32, row_count)
    lower_mask = row_ids[:, None] >= row_ids[None, :]
    decay_matrix = jnp.exp(
        jnp.where(lower_mask, cumulative[:, None] - cumulative[None, :], -jnp.inf)
    )
    weights = (scores * scores * decay_matrix * live_mask[None, :]).astype(jnp.bfloat16)
    local_term = jnp.dot(weights, payload_lines, preferred_element_type=jnp.float32)
    carried_term = carried_read(query_rows, carried, tables)
    running = local_term + jnp.exp(cumulative)[:, None] * carried_term
    return (live_mask[:, None] * rms_rows(running)).astype(jnp.bfloat16)


def on_device(queries, key_rows, values, log_gate, lengths, cont_queries, cont_prompt):
    wide_count = lax.axis_size("wide")
    lane_count = lax.axis_size("narrow")
    owner_index = lax.axis_index("wide")
    prompt_lane = lax.axis_index("narrow")
    query_rows = queries[0]
    own_keys = key_rows[0]
    payload_lines = values[0]
    row_count, head_width = own_keys.shape
    tables = pair_tables(head_width, wide_count)
    lead_all, trail_all, doubled_all = (tables[0], tables[1], tables[2])
    padded_rows = tables[4]
    rows_per = padded_rows // wide_count
    position = owner_index * row_count + lax.iota(jnp.int32, row_count)
    live_mask = (position < lengths[0]).astype(jnp.float32)
    cumulative = jnp.cumsum(log_gate[0] * live_mask)
    piece_number = cumulative[-1]
    scaled = live_mask * jnp.exp(piece_number - cumulative)
    spread = (scaled[:, None] * payload_lines.astype(jnp.float32)).astype(jnp.bfloat16)
    span_state = block_state(own_keys, spread, tables)
    totals = lax.all_gather(piece_number[None], "wide", axis=0, tiled=True)
    sent_slices = lax.all_to_all(
        span_state.reshape(wide_count, rows_per, head_width),
        "wide",
        split_axis=0,
        concat_axis=0,
        tiled=True,
    )
    rounded = owner_prefix(sent_slices, totals).astype(jnp.bfloat16)
    carried_slices = lax.all_to_all(
        rounded[:wide_count], "wide", split_axis=0, concat_axis=0, tiled=True
    )
    carried = carried_slices.reshape(padded_rows, head_width)
    final_slice = rounded[wide_count]
    prompt_out = prompt_rows(
        query_rows, own_keys, payload_lines, cumulative, live_mask, carried, tables
    )
    prompt_ids = lax.iota(jnp.int32, lane_count)[:, None]
    chosen = (cont_prompt[None, :] == prompt_ids)[:, :, None]
    masked = jnp.where(chosen, cont_queries[None, :, :], jnp.zeros_like(cont_queries)[None, :, :])
    pair_rows = lax.all_gather(masked, "narrow", axis=1, tiled=True)
    own_rows = lax.dynamic_index_in_dim(pair_rows, prompt_lane, 0, keepdims=False)
    initial = jnp.zeros((own_rows.shape[0], head_width), jnp.float32)
    shard_portion = lax.all_gather(final_slice, "wide", axis=0, tiled=True)
    piece_rows = shard_portion.shape[0]
    features = pair_block(
        own_rows,
        lax.slice_in_dim(lead_all, 0, piece_rows, axis=0),
        lax.slice_in_dim(trail_all, 0, piece_rows, axis=0),
        lax.slice_in_dim(doubled_all, 0, piece_rows, axis=0),
    )
    partial_value = initial + jnp.dot(features, shard_portion, preferred_element_type=jnp.float32)
    running = lax.psum_scatter(partial_value, "narrow", scatter_dimension=0, tiled=True)
    cont_out = rms_rows(running).astype(jnp.bfloat16)
    return (prompt_out[None], cont_out)


def solution(mesh):
    in_specs = (
        P(("groups", "narrow"), "wide", None),
        P(("groups", "narrow"), "wide", None),
        P(("groups", "narrow"), "wide", None),
        P(("groups", "narrow"), "wide"),
        P(("groups", "narrow")),
        P(("groups", "wide", "narrow"), None),
        P(("groups", "wide", "narrow")),
    )
    out_specs = (P(("groups", "narrow"), "wide", None), P(("groups", "wide", "narrow"), None))
    return jax.shard_map(
        on_device, mesh=mesh, in_specs=in_specs, out_specs=out_specs, check_vma=False
    )
```

profile of v0, /device:TPU:0, one launch (start us, length us, event | category | flops | bytes accessed | tf_op | source)
XLA Modules:
  0.0 162.9 jit_solution(10118833108402280067)
XLA Ops:
  1.3 0.7 compare_select_fusion.4
  2.0 0.3 reduce-window.19
  2.4 0.1 slice_reduce_fusion
  2.6 0.9 copy.25
  3.5 1.2 dynamic-slice
  4.7 1.3 slice_dynamic-update-slice_fusion
  6.0 0.6 exponential_select_fusion
  6.8 33.6 %while.29 = (s32[]{:T(128)}, bf16[3072,64]{0,1:T(8,128)(2,1)S(1)}, bf16[256,64]{0,1:T(8,128)(2,1)}, bf16[256,64]{1,0:T(8,128)(2,1)S(1)}, s32[]{:T(128)}, /*index...) while((s32[]{:T(128)}, bf16[3072,64]{0,1:T(8,128)(2,1)S(1)}, ...), condition=%wide.region_4.6_spmd.clone, body=%wide.region_3.5_spmd.sunk.clone.sunk | while | flops 35475460 | bytes 3522759 | solution.py:68
  6.8 0.7 fusion.85
  7.5 3.9 %gather_fusion = bf16[1024,256]{1,0:T(8,128)(2,1)S(1)} fusion(bf16[256,64]{0,1:T(8,128)(2,1)S(1)} %copy-done.1, s32[1024]{0:T(1024)S(1)} %get-tuple-element.395), kind=kCustom, calls=%fused_computation.2.clone.clone.1 | custom fusion | bytes 1052672 | tf_op jit(solution)/shard_map/while/body/eval_jaxpr/jit(_take)/gather | solution.py:44
  11.5 3.9 %gather_fusion.1 = bf16[1024,256]{1,0:T(8,128)(2,1)S(1)} fusion(bf16[256,64]{0,1:T(8,128)(2,1)S(1)} %copy-done.1, s32[1024]{0:T(1024)S(1)} %get-tuple-element.396), kind=kCustom, calls=%fused_computation.clone.clone.1 | custom fusion | bytes 1052672 | tf_op jit(solution)/shard_map/while/body/eval_jaxpr/jit(_take)/gather | solution.py:43
  15.4 0.7 fusion.86
  16.2 0.7 dynamic_slice.128
  16.8 1.1 fusion.87
  18.0 0.7 fusion.85
  18.8 3.9 %gather_fusion = bf16[1024,256]{1,0:T(8,128)(2,1)S(1)} fusion(bf16[256,64]{0,1:T(8,128)(2,1)S(1)} %copy-done.1, s32[1024]{0:T(1024)S(1)} %get-tuple-element.395), kind=kCustom, calls=%fused_computation.2.clone.clone.1 | custom fusion | bytes 1052672 | tf_op jit(solution)/shard_map/while/body/eval_jaxpr/jit(_take)/gather | solution.py:44
  22.7 3.9 %gather_fusion.1 = bf16[1024,256]{1,0:T(8,128)(2,1)S(1)} fusion(bf16[256,64]{0,1:T(8,128)(2,1)S(1)} %copy-done.1, s32[1024]{0:T(1024)S(1)} %get-tuple-element.396), kind=kCustom, calls=%fused_computation.clone.clone.1 | custom fusion | bytes 1052672 | tf_op jit(solution)/shard_map/while/body/eval_jaxpr/jit(_take)/gather | solution.py:43
  26.6 0.7 fusion.86
  27.4 0.7 dynamic_slice.128
  28.1 1.1 fusion.87
  29.2 0.7 fusion.85
  30.0 3.9 %gather_fusion = bf16[1024,256]{1,0:T(8,128)(2,1)S(1)} fusion(bf16[256,64]{0,1:T(8,128)(2,1)S(1)} %copy-done.1, s32[1024]{0:T(1024)S(1)} %get-tuple-element.395), kind=kCustom, calls=%fused_computation.2.clone.clone.1 | custom fusion | bytes 1052672 | tf_op jit(solution)/shard_map/while/body/eval_jaxpr/jit(_take)/gather | solution.py:44
  33.9 3.9 %gather_fusion.1 = bf16[1024,256]{1,0:T(8,128)(2,1)S(1)} fusion(bf16[256,64]{0,1:T(8,128)(2,1)S(1)} %copy-done.1, s32[1024]{0:T(1024)S(1)} %get-tuple-element.396), kind=kCustom, calls=%fused_computation.clone.clone.1 | custom fusion | bytes 1052672 | tf_op jit(solution)/shard_map/while/body/eval_jaxpr/jit(_take)/gather | solution.py:43
  37.9 0.7 fusion.86
  38.6 0.7 dynamic_slice.128
  39.3 1.1 fusion.87
  40.5 0.5 reshape.156
  41.0 0.8 copy.26
  41.7 7.4 %all-to-all-start = ((bf16[8,260,64]{1,2,0:T(8,128)(2,1)}), bf16[8,260,64]{1,2,0:T(8,128)(2,1)S(1)}, u32[]{:S(2)}, u32[]{:S(2)}) async-start(bf16[8,260,64]{1,2,0:T(8,128)(2,1)} %copy.26), calls=%async_computation | async-start | bytes 786432 | tf_op jit(solution)/shard_map/all_to_all | solution.py:143
  49.3 1.8 %all_gather.10 = bf16[2,10,64]{2,0,1:T(2,128)(2,1)S(1)} all-gather(bf16[2,5,64]{2,0,1:T(2,128)(2,1)S(1)} %broadcast_select_fusion), channel_id=1, replica_groups=mesh['groups'=2,'wide'=8,'narrow'=2] {'narrow'}, dimensions={1}, use_global_device_ids=true | all-gather | bytes 3840 | tf_op jit(solution)/shard_map/all_gather | solution.py:162
  51.2 21.8 %all-reduce.1 = f32[8]{0:T(128)S(1)} all-reduce(f32[8]{0:T(128)S(1)} %get-tuple-element.337), channel_id=1, replica_groups=mesh['groups'=2,'wide'=8,'narrow'=2] {'wide'}, use_global_device_ids=true, to_apply=%add.1 | all-reduce | flops 8 | bytes 64
  73.0 0.2 reduce-window.21
  73.2 0.1 copy.31
  73.3 4.8 %gather_fusion.4 = bf16[2080,10]{1,0:T(8,128)(2,1)S(1)} fusion(bf16[10,64]{0,1:T(8,128)(2,1)S(1)} %bitcast.90, s32[3072]{0:T(1024)S(1)} %pad_clamp_fusion.1), kind=kCustom, calls=%fused_computation.1.clone | custom fusion | bytes 91520 | tf_op jit(solution)/shard_map/jit(_take)/gather | solution.py:43
  78.1 4.8 %gather_fusion.5 = bf16[2080,10]{1,0:T(8,128)(2,1)S(1)} fusion(bf16[10,64]{0,1:T(8,128)(2,1)S(1)} %bitcast.91, s32[3072]{0:T(1024)S(1)} %pad_clamp_fusion), kind=kCustom, calls=%fused_computation.5.clone | custom fusion | bytes 91520 | tf_op jit(solution)/shard_map/jit(_take)/gather | solution.py:44
  82.9 0.6 dynamic-slice.1
  84.2 0.9 convolution_convert_fusion.1
  85.2 0.2 copy.32
  85.4 33.2 %all-gather = bf16[1,2080,64]{2,0,1:T(2,128)(2,1)S(1)} all-gather(bf16[1,260,64]{2,0,1:T(2,128)(2,1)S(1)} %copy.32), channel_id=2, replica_groups=mesh['groups'=2,'wide'=8,'narrow'=2] {'wide'}, dimensions={1}, use_global_device_ids=true | all-gather | bytes 299520 | tf_op jit(solution)/shard_map/all_gather | solution.py:165
  118.6 1.3 copy.33
  119.9 0.8 copy.28
  120.7 3.5 %all-to-all-start.1 = ((bf16[8,260,64]{1,2,0:T(8,128)(2,1)}), bf16[8,260,64]{1,2,0:T(8,128)(2,1)S(1)}, u32[]{:S(2)}, u32[]{:S(2)}) async-start(bf16[8,260,64]{1,2,0:T(8,128)(2,1)} %copy.28), calls=%async_computation.1 | async-start | bytes 786432 | tf_op jit(solution)/shard_map/all_to_all | solution.py:151
  124.2 0.6 fusion.42
  124.8 2.5 %all-reduce.2 = f32[10,64]{1,0:T(8,128)S(1)} all-reduce(f32[10,64]{1,0:T(8,128)S(1)} %fusion.42), channel_id=3, replica_groups=mesh['groups'=2,'wide'=8,'narrow'=2] {'narrow'}, use_global_device_ids=true, to_apply=%region_8.11.clone | all-reduce | flops 640 | bytes 5120
  127.3 0.1 multiply_reduce_fusion.1
  127.4 0.7 multiply_convert_fusion.8
  128.0 5.3 %all-to-all-done.1 = bf16[8,260,64]{1,2,0:T(8,128)(2,1)S(1)} async-done(((bf16[8,260,64]{1,2,0:T(8,128)(2,1)}), bf16[8,260,64]{1,2,0:T(8,128)(2,1)S(1)}, u32[]{:S(2)}, u32[]{:S(2)}) %all-to-all-start.1) | async-done | bytes 266272 | tf_op jit(solution)/shard_map/all_to_all | solution.py:151
  133.3 0.2 copy.29
  133.5 0.3 reshape.157
  133.9 27.9 %while.30 = (s32[]{:T(128)}, f32[256,64]{0,1:T(8,128)S(1)}, bf16[256,64]{0,1:T(8,128)(2,1)S(1)}, bf16[3072,64]{0,1:T(8,128)(2,1)S(1)}, s32[]{:T(128)}, /*index=5...) while((s32[]{:T(128)}, f32[256,64]{0,1:T(8,128)S(1)}, ...), condition=%wide.region_6.8_spmd.clone.clone, body=%wide.region_5.7_spmd.sunk.clone.clone.sunk | while | flops 35442696 | bytes 3457205 | solution.py:88
  134.0 3.9 %gather_fusion.2 = bf16[1024,256]{1,0:T(8,128)(2,1)S(1)} fusion(bf16[256,64]{0,1:T(8,128)(2,1)S(1)} %get-tuple-element.464, s32[1024]{0:T(1024)S(1)} %get-tuple-element.403), kind=kCustom, calls=%fused_computation.4.clone.clone.1 | custom fusion | bytes 1052672 | tf_op jit(solution)/shard_map/while/body/eval_jaxpr/jit(_take)/gather | solution.py:44
  137.9 3.9 %gather_fusion.3 = bf16[1024,256]{1,0:T(8,128)(2,1)S(1)} fusion(bf16[256,64]{0,1:T(8,128)(2,1)S(1)} %get-tuple-element.464, s32[1024]{0:T(1024)S(1)} %get-tuple-element.404), kind=kCustom, calls=%fused_computation.3.clone.clone.1 | custom fusion | bytes 1052672 | tf_op jit(solution)/shard_map/while/body/eval_jaxpr/jit(_take)/gather | solution.py:43
  141.9 0.7 dynamic_slice.132
  142.6 0.6 convolution_add_fusion.2
  143.3 3.9 %gather_fusion.2 = bf16[1024,256]{1,0:T(8,128)(2,1)S(1)} fusion(bf16[256,64]{0,1:T(8,128)(2,1)S(1)} %get-tuple-element.464, s32[1024]{0:T(1024)S(1)} %get-tuple-element.403), kind=kCustom, calls=%fused_computation.4.clone.clone.1 | custom fusion | bytes 1052672 | tf_op jit(solution)/shard_map/while/body/eval_jaxpr/jit(_take)/gather | solution.py:44
  147.2 3.9 %gather_fusion.3 = bf16[1024,256]{1,0:T(8,128)(2,1)S(1)} fusion(bf16[256,64]{0,1:T(8,128)(2,1)S(1)} %get-tuple-element.464, s32[1024]{0:T(1024)S(1)} %get-tuple-element.404), kind=kCustom, calls=%fused_computation.3.clone.clone.1 | custom fusion | bytes 1052672 | tf_op jit(solution)/shard_map/while/body/eval_jaxpr/jit(_take)/gather | solution.py:43
  151.2 0.7 dynamic_slice.132
  151.9 0.6 convolution_add_fusion.2
  152.6 3.9 %gather_fusion.2 = bf16[1024,256]{1,0:T(8,128)(2,1)S(1)} fusion(bf16[256,64]{0,1:T(8,128)(2,1)S(1)} %get-tuple-element.464, s32[1024]{0:T(1024)S(1)} %get-tuple-element.403), kind=kCustom, calls=%fused_computation.4.clone.clone.1 | custom fusion | bytes 1052672 | tf_op jit(solution)/shard_map/while/body/eval_jaxpr/jit(_take)/gather | solution.py:44
  156.5 3.9 %gather_fusion.3 = bf16[1024,256]{1,0:T(8,128)(2,1)S(1)} fusion(bf16[256,64]{0,1:T(8,128)(2,1)S(1)} %get-tuple-element.464, s32[1024]{0:T(1024)S(1)} %get-tuple-element.404), kind=kCustom, calls=%fused_computation.3.clone.clone.1 | custom fusion | bytes 1052672 | tf_op jit(solution)/shard_map/while/body/eval_jaxpr/jit(_take)/gather | solution.py:43
  160.5 0.7 dynamic_slice.132
  161.2 0.6 convolution_add_fusion.2
  161.9 0.4 multiply_reduce_fusion
  162.3 0.6 fusion.55
  (55 shorter events, 1.0 us)
Async XLA Ops:
  6.8 0.8 copy-start.1
  18.0 0.8 copy-start.1
  29.2 0.8 copy-start.1
  40.4 8.7 %copy-start.9 = (s32[5]{0:T(128)S(1)}, s32[5]{0:T(128)}, u32[]{:S(2)}) copy-start(s32[5]{0:T(128)} %param.25) | copy-start | bytes 64
  40.4 8.8 %copy-start.8 = (bf16[5,64]{1,0:T(8,128)(2,1)S(1)}, bf16[5,64]{1,0:T(8,128)(2,1)}, u32[]{:S(2)}) copy-start(bf16[5,64]{1,0:T(8,128)(2,1)} %param.24) | copy-start | bytes 1924
  40.5 32.8 %copy-start.7 = (s32[2080]{0:T(1024)S(1)}, s32[2080]{0:T(1024)}, u32[]{:S(2)}) copy-start(s32[2080]{0:T(1024)} %constant.170) | copy-start | bytes 24964
  40.9 37.1 %copy-start.6 = (s32[2080]{0:T(1024)S(1)}, s32[2080]{0:T(1024)}, u32[]{:S(2)}) copy-start(s32[2080]{0:T(1024)} %constant.171) | copy-start | bytes 24964
  41.7 41.1 %copy-start.11 = (u32[32]{0:T(128)S(1)}, u32[32]{0:T(128)}, u32[]{:S(2)}) copy-start(u32[32]{0:T(128)} %constant.174) | copy-start | bytes 388
  41.7 42.5 %all-to-all-start = ((bf16[8,260,64]{1,2,0:T(8,128)(2,1)}), bf16[8,260,64]{1,2,0:T(8,128)(2,1)S(1)}, u32[]{:S(2)}, u32[]{:S(2)}) async-start(bf16[8,260,64]{1,2,0:T(8,128)(2,1)} %copy.26), calls=%async_computation | async-start | bytes 786432 | tf_op jit(solution)/shard_map/all_to_all | solution.py:143
  119.9 4.3 %copy-start.10 = (f32[2080]{0:T(1024)S(1)}, f32[2080]{0:T(1024)}, u32[]{:S(2)}) copy-start(f32[2080]{0:T(1024)} %constant.145) | copy-start | bytes 24964
  120.7 12.6 %all-to-all-start.1 = ((bf16[8,260,64]{1,2,0:T(8,128)(2,1)}), bf16[8,260,64]{1,2,0:T(8,128)(2,1)S(1)}, u32[]{:S(2)}, u32[]{:S(2)}) async-start(bf16[8,260,64]{1,2,0:T(8,128)(2,1)} %copy.28), calls=%async_computation.1 | async-start | bytes 786432 | tf_op jit(solution)/shard_map/all_to_all | solution.py:151
  128.0 5.8 %copy-start = (bf16[1,256,64]{1,2,0:T(8,128)(2,1)S(1)}, bf16[1,256,64]{1,2,0:T(8,128)(2,1)}, u32[]{:S(2)}) copy-start(bf16[1,256,64]{1,2,0:T(8,128)(2,1)} %param.19) | copy-start | bytes 98308
  128.0 5.8 %copy-start.3 = (s32[3072]{0:T(1024)S(1)}, s32[3072]{0:T(1024)}, u32[]{:S(2)}) copy-start(s32[3072]{0:T(1024)} %get-tuple-element.477) | copy-start | bytes 36868
  128.0 5.8 %copy-start.4 = (s32[3072]{0:T(1024)S(1)}, s32[3072]{0:T(1024)}, u32[]{:S(2)}) copy-start(s32[3072]{0:T(1024)} %get-tuple-element.478) | copy-start | bytes 36868
  133.9 27.9 %copy-start.2 = (bf16[256,64]{0,1:T(8,128)(2,1)S(1)}, bf16[256,64]{0,1:T(8,128)(2,1)}, u32[]{:S(2)}) copy-start(bf16[256,64]{0,1:T(8,128)(2,1)} %get-tuple-element.474) | copy-start | bytes 98308
  133.9 27.9 %copy-start.5 = (bf16[1,256,64]{1,2,0:T(8,128)(2,1)S(1)}, bf16[1,256,64]{1,2,0:T(8,128)(2,1)}, u32[]{:S(2)}) copy-start(bf16[1,256,64]{1,2,0:T(8,128)(2,1)} %param.21) | copy-start | bytes 98308
where the time goes:
time: 164 us; the launch traced here: 163 us
  local copies, waits for them, and re-layouts  69.6 us (42%)
  blocking collectives  59.3 us (36%)
  starting transfers between devices  10.9 us (7%)
  other arithmetic  8.08 us (5%)
  matrix products  7.18 us (4%)
  waiting for transfers between devices  5.25 us (3%)
  between operations  2.25 us (1%)
    all_gather x1, blocking collectives, on_device(): shard_portion = lax.all_gather(final_slice, 'wide', axis=0, tiled=True)  33.2 us
    gather x7, local copies, waits for them, and re-layouts, pair_block(): leading_columns = jnp.take(rows, lead_part, axis=1).astype(jnp.float32)  28.4 us
    gather x7, local copies, waits for them, and re-layouts, pair_block(): right_cols = jnp.take(rows, trail_part, axis=1).astype(jnp.float32)  28.4 us
    unnamed x2, blocking collectives  24.3 us
    all_to_all x1, starting transfers between devices, on_device(): lax.all_to_all(span_state.reshape(wide_count, rows_per, head_width), 'wid...  7.41 us
    all_to_all x1, waiting for transfers between devices, on_device(): lax.all_to_all(rounded[:wide_count], 'wide', split_axis=0, concat_axis=0,...  5.25 us
    unnamed x27, local copies, waits for them, and re-layouts  4.03 us
    all_to_all x1, starting transfers between devices, on_device(): lax.all_to_all(rounded[:wide_count], 'wide', split_axis=0, concat_axis=0,...  3.45 us
  transfers between devices with their start and end apart: 2, of which 1 were waited for; matrix products, arithmetic and copies ran while one was open for 7% of the time, Pallas kernels for 0%

commit v1 on v0

--- a/solution.py
+++ b/solution.py
@@ -6,6 +6,22 @@
 
 epsilon = 1e-06
 block_rows = 1024
+
+
+def collect(x, axis, dim):
+    ways, here, hop = (lax.axis_size(axis), lax.axis_index(axis), x.shape[dim])
+    shape = [n * ways if d == dim else n for d, n in enumerate(x.shape)]
+    full = lax.dynamic_update_slice_in_dim(jnp.zeros(shape, x.dtype), x, here * hop, axis=dim)
+    going_up = going_down = x
+    for far in range(1, ways // 2 + 1):
+        going_up = lax.ppermute(going_up, axis, [(d, (d + 1) % ways) for d in range(ways)])
+        full = lax.dynamic_update_slice_in_dim(full, going_up, (here - far) % ways * hop, axis=dim)
+        if 2 * far < ways:
+            going_down = lax.ppermute(going_down, axis, [(d, (d - 1) % ways) for d in range(ways)])
+            full = lax.dynamic_update_slice_in_dim(
+                full, going_down, (here + far) % ways * hop, axis=dim
+            )
+    return full
 
 
 def rms_rows(running):
@@ -162,7 +178,7 @@
     pair_rows = lax.all_gather(masked, "narrow", axis=1, tiled=True)
     own_rows = lax.dynamic_index_in_dim(pair_rows, prompt_lane, 0, keepdims=False)
     initial = jnp.zeros((own_rows.shape[0], head_width), jnp.float32)
-    shard_portion = lax.all_gather(final_slice, "wide", axis=0, tiled=True)
+    shard_portion = collect(final_slice, "wide", 0)
     piece_rows = shard_portion.shape[0]
     features = pair_block(
         own_rows,

time: 164 us -> 152 us (0.927)
  blocking collectives: 59.3 us -> 26.4 us
  starting transfers between devices: 10.9 us -> 28 us
  local copies, waits for them, and re-layouts: 69.6 us -> 74.1 us
    all_gather x1 -> x0, blocking collectives: 33.2 us -> none  [on_device(): shard_portion = lax.all_gather(final_slice, 'wide', axis=0, tiled=True)]
    ppermute x0 -> x7, starting transfers between devices: none -> 14.6 us  [the longest x3 13.6 us: collect(): lax.ppermute(going_down, axis, [(d, (d - 1) % ways) for d in range(ways)])]
    dynamic_update_slice x0 -> x8, local copies, waits for them, and re-layouts: none -> 5.39 us  [the longest x4 2.71 us: collect(): lax.dynamic_update_slice_in_dim(full, going_up, (here - far) % ways * hop...]
    all_to_all x1, waiting for transfers between devices: 5.25 us -> 0.74 us  [on_device(): lax.all_to_all(rounded[:wide_count], 'wide', split_axis=0, concat_axis=0,...]
    ppermute x0 -> x7, waiting for transfers between devices: none -> 4.05 us  [the longest x4 2.48 us: collect(): lax.ppermute(going_up, axis, [(d, (d + 1) % ways) for d in range(ways)])]
    all_to_all x1, starting transfers between devices: 3.45 us -> 6.04 us  [on_device(): lax.all_to_all(rounded[:wide_count], 'wide', split_axis=0, concat_axis=0,...]
    unnamed x27 -> x28, local copies, waits for them, and re-layouts: 4.03 us -> 4.56 us
  transfers between devices with their start and end apart: 2 -> 9, of which waited for: 1 -> 5; matrix products, arithmetic and copies ran while one was open for 7% -> 12% of each run, Pallas kernels for 0% -> 0%
where the time goes in v1:
time: 152 us; the launch traced here: 151 us
  local copies, waits for them, and re-layouts  74.1 us (49%)
  starting transfers between devices  28 us (18%)
  blocking collectives  26.4 us (17%)
  other arithmetic  8.08 us (5%)
  matrix products  7.19 us (5%)
  waiting for transfers between devices  4.79 us (3%)
  between operations  2.41 us (2%)
    gather x7, local copies, waits for them, and re-layouts, pair_block(): leading_columns = jnp.take(rows, lead_part, axis=1).astype(jnp.float32)  28.4 us
    gather x7, local copies, waits for them, and re-layouts, pair_block(): right_cols = jnp.take(rows, trail_part, axis=1).astype(jnp.float32)  28.4 us
    unnamed x2, blocking collectives  24.5 us
    ppermute x3, starting transfers between devices, collect(): lax.ppermute(going_down, axis, [(d, (d - 1) % ways) for d in range(ways)])  13.6 us
    all_to_all x1, starting transfers between devices, on_device(): lax.all_to_all(span_state.reshape(wide_count, rows_per, head_width), 'wid...  7.28 us
    all_to_all x1, starting transfers between devices, on_device(): lax.all_to_all(rounded[:wide_count], 'wide', split_axis=0, concat_axis=0,...  6.04 us
    unnamed x28, local copies, waits for them, and re-layouts  4.56 us
    dot_general x3, matrix products, fill_block(): lax.dot_general(features, spread, (((0,), (0,)), ((), ())), preferred_ele...  3.39 us
  transfers between devices with their start and end apart: 9, of which 5 were waited for; matrix products, arithmetic and copies ran while one was open for 12% of the time, Pallas kernels for 0%

profile of v1, /device:TPU:0, one launch (start us, length us, event | category | flops | bytes accessed | tf_op | source)
XLA Modules:
  0.0 151.2 jit_solution(14769203663458236600)
XLA Ops:
  1.3 0.7 compare_select_fusion.4
  2.6 0.9 copy.23
  3.5 1.3 dynamic-slice
  4.8 1.3 slice_dynamic-update-slice_fusion
  6.1 0.6 exponential_select_fusion
  6.9 33.6 %while.29 = (s32[]{:T(128)}, bf16[3072,64]{0,1:T(8,128)(2,1)S(1)}, bf16[256,64]{0,1:T(8,128)(2,1)}, bf16[256,64]{1,0:T(8,128)(2,1)S(1)}, s32[]{:T(128)}, /*index...) while((s32[]{:T(128)}, bf16[3072,64]{0,1:T(8,128)(2,1)S(1)}, ...), condition=%wide.region_4.6_spmd.clone, body=%wide.region_3.5_spmd.sunk.clone.sunk | while | flops 35475460 | bytes 3522759 | solution.py:84
  6.9 0.7 fusion.85
  7.7 3.9 %gather_fusion = bf16[1024,256]{1,0:T(8,128)(2,1)S(1)} fusion(bf16[256,64]{0,1:T(8,128)(2,1)S(1)} %copy-done.1, s32[1024]{0:T(1024)S(1)} %get-tuple-element.395), kind=kCustom, calls=%fused_computation.2.clone.clone.1 | custom fusion | bytes 1052672 | tf_op jit(solution)/shard_map/while/body/eval_jaxpr/jit(_take)/gather | solution.py:60
  11.6 3.9 %gather_fusion.1 = bf16[1024,256]{1,0:T(8,128)(2,1)S(1)} fusion(bf16[256,64]{0,1:T(8,128)(2,1)S(1)} %copy-done.1, s32[1024]{0:T(1024)S(1)} %get-tuple-element.396), kind=kCustom, calls=%fused_computation.clone.clone.1 | custom fusion | bytes 1052672 | tf_op jit(solution)/shard_map/while/body/eval_jaxpr/jit(_take)/gather | solution.py:59
  15.6 0.7 fusion.86
  16.3 0.7 dynamic_slice.128
  17.0 1.1 fusion.87
  18.1 0.7 fusion.85
  18.9 3.9 %gather_fusion = bf16[1024,256]{1,0:T(8,128)(2,1)S(1)} fusion(bf16[256,64]{0,1:T(8,128)(2,1)S(1)} %copy-done.1, s32[1024]{0:T(1024)S(1)} %get-tuple-element.395), kind=kCustom, calls=%fused_computation.2.clone.clone.1 | custom fusion | bytes 1052672 | tf_op jit(solution)/shard_map/while/body/eval_jaxpr/jit(_take)/gather | solution.py:60
  22.8 3.9 %gather_fusion.1 = bf16[1024,256]{1,0:T(8,128)(2,1)S(1)} fusion(bf16[256,64]{0,1:T(8,128)(2,1)S(1)} %copy-done.1, s32[1024]{0:T(1024)S(1)} %get-tuple-element.396), kind=kCustom, calls=%fused_computation.clone.clone.1 | custom fusion | bytes 1052672 | tf_op jit(solution)/shard_map/while/body/eval_jaxpr/jit(_take)/gather | solution.py:59
  26.8 0.7 fusion.86
  27.5 0.7 dynamic_slice.128
  28.2 1.1 fusion.87
  29.3 0.7 fusion.85
  30.1 3.9 %gather_fusion = bf16[1024,256]{1,0:T(8,128)(2,1)S(1)} fusion(bf16[256,64]{0,1:T(8,128)(2,1)S(1)} %copy-done.1, s32[1024]{0:T(1024)S(1)} %get-tuple-element.395), kind=kCustom, calls=%fused_computation.2.clone.clone.1 | custom fusion | bytes 1052672 | tf_op jit(solution)/shard_map/while/body/eval_jaxpr/jit(_take)/gather | solution.py:60
  34.0 3.9 %gather_fusion.1 = bf16[1024,256]{1,0:T(8,128)(2,1)S(1)} fusion(bf16[256,64]{0,1:T(8,128)(2,1)S(1)} %copy-done.1, s32[1024]{0:T(1024)S(1)} %get-tuple-element.396), kind=kCustom, calls=%fused_computation.clone.clone.1 | custom fusion | bytes 1052672 | tf_op jit(solution)/shard_map/while/body/eval_jaxpr/jit(_take)/gather | solution.py:59
  38.0 0.7 fusion.86
  38.7 0.7 dynamic_slice.128
  39.4 1.1 fusion.87
  41.1 0.8 copy.24
  41.8 7.3 %all-to-all-start = ((bf16[8,260,64]{1,2,0:T(8,128)(2,1)}), bf16[8,260,64]{1,2,0:T(8,128)(2,1)S(1)}, u32[]{:S(2)}, u32[]{:S(2)}) async-start(bf16[8,260,64]{1,2,0:T(8,128)(2,1)} %copy.24), calls=%async_computation | async-start | bytes 786432 | tf_op jit(solution)/shard_map/all_to_all | solution.py:159
  49.1 22.1 %all-reduce.1 = f32[8]{0:T(128)S(1)} all-reduce(f32[8]{0:T(128)S(1)} %get-tuple-element.337), channel_id=1, replica_groups=mesh['groups'=2,'wide'=8,'narrow'=2] {'wide'}, use_global_device_ids=true, to_apply=%add.1 | all-reduce | flops 8 | bytes 64
  71.6 0.9 convolution_convert_fusion.1
  72.6 1.0 collective-permute-start
  73.7 3.8 %collective-permute-start.1 = (bf16[260,64]{0,1:T(8,128)(2,1)S(1)}, bf16[260,64]{0,1:T(8,128)(2,1)S(1)}, u32[]{:S(2)}, u32[]{:S(2)}) collective-permute-start(bf16[260,64]{0,1:T(8,128)(2,1)S(1)} %bitcast.94), channel_id=1, source_target_pairs={{0,14},{2,0},{4,2},{6,4},{8,6},{10,8},{12,10},{14,12},{1,15},{3,1}... | collective-permute-start | bytes 99848 | tf_op jit(solution)/shard_map/ppermute | solution.py:20
  77.5 2.1 %collective-permute-done = bf16[260,64]{0,1:T(8,128)(2,1)S(1)} collective-permute-done((bf16[260,64]{0,1:T(8,128)(2,1)S(1)}, bf16[260,64]{0,1:T(8,128)(2,1)S(1)}, u32[]{:S(2)}, u32[]{:S(2)}) %collective-permute-start) | collective-permute-done | bytes 33312 | tf_op jit(solution)/shard_map/ppermute | solution.py:17
  79.6 1.8 %all_gather.7 = bf16[2,10,64]{2,0,1:T(2,128)(2,1)S(1)} all-gather(bf16[2,5,64]{2,0,1:T(2,128)(2,1)S(1)} %broadcast_select_fusion), channel_id=1, replica_groups=mesh['groups'=2,'wide'=8,'narrow'=2] {'narrow'}, dimensions={1}, use_global_device_ids=true | all-gather | bytes 3840 | tf_op jit(solution)/shard_map/all_gather | solution.py:178
  81.5 4.8 %collective-permute-start.3 = (bf16[260,64]{0,1:T(8,128)(2,1)S(1)}, bf16[260,64]{0,1:T(8,128)(2,1)S(1)}, u32[]{:S(2)}, u32[]{:S(2)}) collective-permute-start(bf16[260,64]{0,1:T(8,128)(2,1)S(1)} %collective-permute-done.1), channel_id=1, source_target_pairs={{0,14},{2,0},{4,2},{6,4},{8,6},{10,8},{12,10},{14,12},{1,15},{3,1}... | collective-permute-start | bytes 99848 | tf_op jit(solution)/shard_map/ppermute | solution.py:20
  86.4 1.6 %collective-permute-done.3 = bf16[260,64]{0,1:T(8,128)(2,1)S(1)} collective-permute-done((bf16[260,64]{0,1:T(8,128)(2,1)S(1)}, bf16[260,64]{0,1:T(8,128)(2,1)S(1)}, u32[]{:S(2)}, u32[]{:S(2)}) %collective-permute-start.3) | collective-permute-done | bytes 33312 | tf_op jit(solution)/shard_map/ppermute | solution.py:20
  88.0 5.0 %collective-permute-start.5 = (bf16[260,64]{0,1:T(8,128)(2,1)S(1)}, bf16[260,64]{0,1:T(8,128)(2,1)S(1)}, u32[]{:S(2)}, u32[]{:S(2)}) collective-permute-start(bf16[260,64]{0,1:T(8,128)(2,1)S(1)} %collective-permute-done.3), channel_id=1, source_target_pairs={{0,14},{2,0},{4,2},{6,4},{8,6},{10,8},{12,10},{14,12},{1,15},{3,1}... | collective-permute-start | bytes 99848 | tf_op jit(solution)/shard_map/ppermute | solution.py:20
  93.4 4.8 %gather_fusion.4 = bf16[2080,10]{1,0:T(8,128)(2,1)S(1)} fusion(bf16[10,64]{0,1:T(8,128)(2,1)S(1)} %bitcast.91, s32[3072]{0:T(1024)S(1)} %pad_clamp_fusion.1), kind=kCustom, calls=%fused_computation.1.clone | custom fusion | bytes 91520 | tf_op jit(solution)/shard_map/jit(_take)/gather | solution.py:59
  98.2 4.8 %gather_fusion.5 = bf16[2080,10]{1,0:T(8,128)(2,1)S(1)} fusion(bf16[10,64]{0,1:T(8,128)(2,1)S(1)} %bitcast.92, s32[3072]{0:T(1024)S(1)} %pad_clamp_fusion), kind=kCustom, calls=%fused_computation.5.clone | custom fusion | bytes 91520 | tf_op jit(solution)/shard_map/jit(_take)/gather | solution.py:60
  103.0 0.6 dynamic-slice.1
  104.3 0.8 copy.26
  105.1 6.0 %all-to-all-start.1 = ((bf16[8,260,64]{1,2,0:T(8,128)(2,1)}), bf16[8,260,64]{1,2,0:T(8,128)(2,1)S(1)}, u32[]{:S(2)}, u32[]{:S(2)}) async-start(bf16[8,260,64]{1,2,0:T(8,128)(2,1)} %copy.26), calls=%async_computation.1 | async-start | bytes 786432 | tf_op jit(solution)/shard_map/all_to_all | solution.py:167
  112.2 0.7 dynamic_update_slice.33
  113.0 0.7 dynamic_update_slice.34
  113.7 0.7 dynamic_update_slice.35
  114.4 0.7 dynamic_update_slice.36
  115.1 0.7 dynamic_update_slice.37
  115.9 0.7 dynamic_update_slice.38
  116.6 0.6 fusion.42
  117.2 2.5 %all-reduce.2 = f32[10,64]{1,0:T(8,128)S(1)} all-reduce(f32[10,64]{1,0:T(8,128)S(1)} %fusion.42), channel_id=2, replica_groups=mesh['groups'=2,'wide'=8,'narrow'=2] {'narrow'}, use_global_device_ids=true, to_apply=%region_8.11.clone | all-reduce | flops 640 | bytes 5120
  119.8 0.7 multiply_convert_fusion.8
  120.5 0.7 all-to-all-done.1
  122.2 27.9 %while.30 = (s32[]{:T(128)}, f32[256,64]{0,1:T(8,128)S(1)}, bf16[256,64]{0,1:T(8,128)(2,1)S(1)}, bf16[3072,64]{0,1:T(8,128)(2,1)S(1)}, s32[]{:T(128)}, /*index=5...) while((s32[]{:T(128)}, f32[256,64]{0,1:T(8,128)S(1)}, ...), condition=%wide.region_6.8_spmd.clone.clone, body=%wide.region_5.7_spmd.sunk.clone.clone.sunk | while | flops 35442696 | bytes 3457205 | solution.py:104
  122.3 3.9 %gather_fusion.2 = bf16[1024,256]{1,0:T(8,128)(2,1)S(1)} fusion(bf16[256,64]{0,1:T(8,128)(2,1)S(1)} %get-tuple-element.464, s32[1024]{0:T(1024)S(1)} %get-tuple-element.403), kind=kCustom, calls=%fused_computation.4.clone.clone.1 | custom fusion | bytes 1052672 | tf_op jit(solution)/shard_map/while/body/eval_jaxpr/jit(_take)/gather | solution.py:60
  126.2 3.9 %gather_fusion.3 = bf16[1024,256]{1,0:T(8,128)(2,1)S(1)} fusion(bf16[256,64]{0,1:T(8,128)(2,1)S(1)} %get-tuple-element.464, s32[1024]{0:T(1024)S(1)} %get-tuple-element.404), kind=kCustom, calls=%fused_computation.3.clone.clone.1 | custom fusion | bytes 1052672 | tf_op jit(solution)/shard_map/while/body/eval_jaxpr/jit(_take)/gather | solution.py:59
  130.2 0.7 dynamic_slice.132
  130.9 0.6 convolution_add_fusion.2
  131.6 3.9 %gather_fusion.2 = bf16[1024,256]{1,0:T(8,128)(2,1)S(1)} fusion(bf16[256,64]{0,1:T(8,128)(2,1)S(1)} %get-tuple-element.464, s32[1024]{0:T(1024)S(1)} %get-tuple-element.403), kind=kCustom, calls=%fused_computation.4.clone.clone.1 | custom fusion | bytes 1052672 | tf_op jit(solution)/shard_map/while/body/eval_jaxpr/jit(_take)/gather | solution.py:60
  135.5 3.9 %gather_fusion.3 = bf16[1024,256]{1,0:T(8,128)(2,1)S(1)} fusion(bf16[256,64]{0,1:T(8,128)(2,1)S(1)} %get-tuple-element.464, s32[1024]{0:T(1024)S(1)} %get-tuple-element.404), kind=kCustom, calls=%fused_computation.3.clone.clone.1 | custom fusion | bytes 1052672 | tf_op jit(solution)/shard_map/while/body/eval_jaxpr/jit(_take)/gather | solution.py:59
  139.5 0.7 dynamic_slice.132
  140.2 0.6 convolution_add_fusion.2
  140.9 3.9 %gather_fusion.2 = bf16[1024,256]{1,0:T(8,128)(2,1)S(1)} fusion(bf16[256,64]{0,1:T(8,128)(2,1)S(1)} %get-tuple-element.464, s32[1024]{0:T(1024)S(1)} %get-tuple-element.403), kind=kCustom, calls=%fused_computation.4.clone.clone.1 | custom fusion | bytes 1052672 | tf_op jit(solution)/shard_map/while/body/eval_jaxpr/jit(_take)/gather | solution.py:60
  144.8 3.9 %gather_fusion.3 = bf16[1024,256]{1,0:T(8,128)(2,1)S(1)} fusion(bf16[256,64]{0,1:T(8,128)(2,1)S(1)} %get-tuple-element.464, s32[1024]{0:T(1024)S(1)} %get-tuple-element.404), kind=kCustom, calls=%fused_computation.3.clone.clone.1 | custom fusion | bytes 1052672 | tf_op jit(solution)/shard_map/while/body/eval_jaxpr/jit(_take)/gather | solution.py:59
  148.8 0.7 dynamic_slice.132
  149.5 0.6 convolution_add_fusion.2
  150.6 0.6 fusion.54
  (76 shorter events, 5.0 us)
Async XLA Ops:
  6.9 0.8 copy-start.1
  18.1 0.8 copy-start.1
  29.3 0.8 copy-start.1
  41.0 30.4 %copy-start.9 = (s32[5]{0:T(128)S(1)}, s32[5]{0:T(128)}, u32[]{:S(2)}) copy-start(s32[5]{0:T(128)} %param.25) | copy-start | bytes 64
  41.0 30.5 %copy-start.8 = (bf16[5,64]{1,0:T(8,128)(2,1)S(1)}, bf16[5,64]{1,0:T(8,128)(2,1)}, u32[]{:S(2)}) copy-start(bf16[5,64]{1,0:T(8,128)(2,1)} %param.24) | copy-start | bytes 1924
  41.8 29.8 %all-to-all-start = ((bf16[8,260,64]{1,2,0:T(8,128)(2,1)}), bf16[8,260,64]{1,2,0:T(8,128)(2,1)S(1)}, u32[]{:S(2)}, u32[]{:S(2)}) async-start(bf16[8,260,64]{1,2,0:T(8,128)(2,1)} %copy.24), calls=%async_computation | async-start | bytes 786432 | tf_op jit(solution)/shard_map/all_to_all | solution.py:159
  49.1 24.5 %copy-start.7 = (s32[2080]{0:T(1024)S(1)}, s32[2080]{0:T(1024)}, u32[]{:S(2)}) copy-start(s32[2080]{0:T(1024)} %constant.225) | copy-start | bytes 24964
  49.1 30.5 %copy-start.6 = (s32[2080]{0:T(1024)S(1)}, s32[2080]{0:T(1024)}, u32[]{:S(2)}) copy-start(s32[2080]{0:T(1024)} %constant.226) | copy-start | bytes 24964
  72.6 7.0 %collective-permute-start = (bf16[260,64]{0,1:T(8,128)(2,1)S(1)}, bf16[260,64]{0,1:T(8,128)(2,1)S(1)}, u32[]{:S(2)}, u32[]{:S(2)}) collective-permute-start(bf16[260,64]{0,1:T(8,128)(2,1)S(1)} %bitcast.93), channel_id=1, source_target_pairs={{0,2},{2,4},{4,6},{6,8},{8,10},{10,12},{12,14},{14,0},{1,3},{3,5},... | collective-permute-start | bytes 99848 | tf_op jit(solution)/shard_map/ppermute | solution.py:17
  73.7 7.8 %collective-permute-start.1 = (bf16[260,64]{0,1:T(8,128)(2,1)S(1)}, bf16[260,64]{0,1:T(8,128)(2,1)S(1)}, u32[]{:S(2)}, u32[]{:S(2)}) collective-permute-start(bf16[260,64]{0,1:T(8,128)(2,1)S(1)} %bitcast.94), channel_id=1, source_target_pairs={{0,14},{2,0},{4,2},{6,4},{8,6},{10,8},{12,10},{14,12},{1,15},{3,1}... | collective-permute-start | bytes 99848 | tf_op jit(solution)/shard_map/ppermute | solution.py:20
  79.6 6.8 %collective-permute-start.2 = (bf16[260,64]{0,1:T(8,128)(2,1)S(1)}, bf16[260,64]{0,1:T(8,128)(2,1)S(1)}, u32[]{:S(2)}, u32[]{:S(2)}) collective-permute-start(bf16[260,64]{0,1:T(8,128)(2,1)S(1)} %collective-permute-done), channel_id=1, source_target_pairs={{0,2},{2,4},{4,6},{6,8},{8,10},{10,12},{12,14},{14,0},{1,3},{3,5},... | collective-permute-start | bytes 99848 | tf_op jit(solution)/shard_map/ppermute | solution.py:17
  81.5 21.5 %copy-start.11 = (u32[32]{0:T(128)S(1)}, u32[32]{0:T(128)}, u32[]{:S(2)}) copy-start(u32[32]{0:T(128)} %constant.229) | copy-start | bytes 388
  81.5 6.5 %collective-permute-start.3 = (bf16[260,64]{0,1:T(8,128)(2,1)S(1)}, bf16[260,64]{0,1:T(8,128)(2,1)S(1)}, u32[]{:S(2)}, u32[]{:S(2)}) collective-permute-start(bf16[260,64]{0,1:T(8,128)(2,1)S(1)} %collective-permute-done.1), channel_id=1, source_target_pairs={{0,14},{2,0},{4,2},{6,4},{8,6},{10,8},{12,10},{14,12},{1,15},{3,1}... | collective-permute-start | bytes 99848 | tf_op jit(solution)/shard_map/ppermute | solution.py:20
  86.4 6.8 %collective-permute-start.4 = (bf16[260,64]{0,1:T(8,128)(2,1)S(1)}, bf16[260,64]{0,1:T(8,128)(2,1)S(1)}, u32[]{:S(2)}, u32[]{:S(2)}) collective-permute-start(bf16[260,64]{0,1:T(8,128)(2,1)S(1)} %collective-permute-done.2), channel_id=1, source_target_pairs={{0,2},{2,4},{4,6},{6,8},{8,10},{10,12},{12,14},{14,0},{1,3},{3,5},... | collective-permute-start | bytes 99848 | tf_op jit(solution)/shard_map/ppermute | solution.py:17
  88.0 27.1 %collective-permute-start.5 = (bf16[260,64]{0,1:T(8,128)(2,1)S(1)}, bf16[260,64]{0,1:T(8,128)(2,1)S(1)}, u32[]{:S(2)}, u32[]{:S(2)}) collective-permute-start(bf16[260,64]{0,1:T(8,128)(2,1)S(1)} %collective-permute-done.3), channel_id=1, source_target_pairs={{0,14},{2,0},{4,2},{6,4},{8,6},{10,8},{12,10},{14,12},{1,15},{3,1}... | collective-permute-start | bytes 99848 | tf_op jit(solution)/shard_map/ppermute | solution.py:20
  93.2 22.7 %collective-permute-start.6 = (bf16[260,64]{0,1:T(8,128)(2,1)S(1)}, bf16[260,64]{0,1:T(8,128)(2,1)S(1)}, u32[]{:S(2)}, u32[]{:S(2)}) collective-permute-start(bf16[260,64]{0,1:T(8,128)(2,1)S(1)} %collective-permute-done.4), channel_id=1, source_target_pairs={{0,2},{2,4},{4,6},{6,8},{8,10},{10,12},{12,14},{14,0},{1,3},{3,5},... | collective-permute-start | bytes 99848 | tf_op jit(solution)/shard_map/ppermute | solution.py:17
  105.1 11.5 %copy-start.10 = (f32[2080]{0:T(1024)S(1)}, f32[2080]{0:T(1024)}, u32[]{:S(2)}) copy-start(f32[2080]{0:T(1024)} %constant.200) | copy-start | bytes 24964
  105.1 16.2 %all-to-all-start.1 = ((bf16[8,260,64]{1,2,0:T(8,128)(2,1)}), bf16[8,260,64]{1,2,0:T(8,128)(2,1)S(1)}, u32[]{:S(2)}, u32[]{:S(2)}) async-start(bf16[8,260,64]{1,2,0:T(8,128)(2,1)} %copy.26), calls=%async_computation.1 | async-start | bytes 786432 | tf_op jit(solution)/shard_map/all_to_all | solution.py:167
  121.5 0.8 copy-start
  121.5 0.8 copy-start.3
  121.5 0.7 copy-start.4
  122.2 27.9 %copy-start.2 = (bf16[256,64]{0,1:T(8,128)(2,1)S(1)}, bf16[256,64]{0,1:T(8,128)(2,1)}, u32[]{:S(2)}) copy-start(bf16[256,64]{0,1:T(8,128)(2,1)} %get-tuple-element.474) | copy-start | bytes 98308
  122.2 27.9 %copy-start.5 = (bf16[1,256,64]{1,2,0:T(8,128)(2,1)S(1)}, bf16[1,256,64]{1,2,0:T(8,128)(2,1)}, u32[]{:S(2)}) copy-start(bf16[1,256,64]{1,2,0:T(8,128)(2,1)} %param.21) | copy-start | bytes 98308
